TPU v7x, 32 devices: a whole 2x2x4 slice. The times are simulated.
32 devices in a mesh: dp: 8 (over z, y), tensor: 4 (over x, core).
Axes of the slice: x: 2, y: 2, z: 4, core: 2. Of those that a mesh axis runs over, the one named last changes fastest.
Arguments:
- tokens: bfloat16 [1024, 16, 768], P(('dp', 'tensor')), may hold values from -6 to 6
- lengths: int32 [16], replicated, may hold values from 1 to 1024, 12288 in all
- dealing: int32 [16], replicated, may hold values from 0 to 15, each once
- project_weight: bfloat16 [768, 2304], P('dp', 'tensor'), may hold values from -0.21875 to 0.21875
- query_projection_bias: float32 [768], replicated, may hold values from -3 to 3
- value_projection_bias: float32 [768], replicated, may hold values from -3 to 3
- attention_output_weight: bfloat16 [768, 768], P('dp', 'tensor'), may hold values from -3.5 to 3.5
- attention_output_bias: float32 [768], replicated, may hold values from -3 to 3
- first_gain: float32 [768], replicated, may hold values from 0.5 to 1.5
- first_shift: float32 [768], replicated, may hold values from -3 to 3
- feed_input_weight: bfloat16 [768, 3072], P('dp', 'tensor'), may hold values from -0.21875 to 0.21875
- feed_input_bias: float32 [3072], replicated, may hold values from -3 to 3
- feed_output_weight: bfloat16 [768, 3072], P('dp', 'tensor'), may hold values from -0.109375 to 0.109375
- feed_output_bias: float32 [768], replicated, may hold values from -3 to 3
- second_gain: float32 [768], replicated, may hold values from 0.5 to 1.5
- second_shift: float32 [768], replicated, may hold values from -3 to 3
- output_grad: bfloat16 [1024, 16, 768], P(('dp', 'tensor')), may hold values from -6 to 6
Outputs:
- layer_output: bfloat16 [1024, 16, 768], P('tensor', 'dp')
- tokens_grad: bfloat16 [1024, 16, 768], P(('dp', 'tensor'))
- project_grad: float32 [768, 2304], P('dp', 'tensor')
- query_bias_grad: float32 [768], P(('dp', 'tensor'))
- value_bias_grad: float32 [768], P(('dp', 'tensor'))
- output_weight_grad: float32 [768, 768], P('dp', 'tensor')
- output_bias_grad: float32 [768], P(('dp', 'tensor'))
- first_gain_grad: float32 [768], P(('dp', 'tensor'))
- first_shift_grad: float32 [768], P(('dp', 'tensor'))
- up_weight_grad: float32 [768, 3072], P('dp', 'tensor')
- up_bias_grad: float32 [3072], P(('dp', 'tensor'))
- down_weight_grad: float32 [768, 3072], P('dp', 'tensor')
- down_bias_grad: float32 [768], P(('dp', 'tensor'))
- second_gain_grad: float32 [768], P(('dp', 'tensor'))
- second_shift_grad: float32 [768], P(('dp', 'tensor'))
Inputs may be any that keep to these rules, and one draw needn't show every extreme that they name: `lengths`: the longest sequence has exactly 1024 tokens. A permutation: sequence s is processed in slot dealing[s], and slot q belongs to data index q // 2.
All inputs are finite; a program needn't handle non-finite values.
Results may differ from a plain program's by a relative error of at most 0.022.
Values may be sent and summed in bfloat16 or wider, within the bound.
A program may use at most 128 MiB of HBM per device.

v0:
```python
from functools import partial
import jax
import jax.numpy as jnp
from jax import lax
from jax.sharding import PartitionSpec as P

HD = 64
EPSILON = 1e-12
MASKED = -1e30


def norm_forward(value, gain, shift):
    centred = value - jnp.mean(value, axis=-1, keepdims=True)
    inverse = lax.rsqrt(jnp.mean(centred * centred, axis=-1, keepdims=True) + EPSILON)
    normed = centred * inverse
    return (normed * gain + shift, normed, inverse)


def norm_backward(upstream, normed, inverse, gain):
    scaled = upstream * gain
    first_mean = jnp.mean(scaled, axis=-1, keepdims=True)
    second_mean = jnp.mean(scaled * normed, axis=-1, keepdims=True)
    return inverse * (scaled - first_mean - normed * second_mean)


def spread_block(values, block_index, length_total):
    blank = jnp.zeros((length_total,), jnp.float32)
    return lax.dynamic_update_slice_in_dim(blank, values, block_index * values.shape[0], 0)


def gather_rows(block):
    return lax.all_gather(block, "tensor", axis=0, tiled=True)


def scatter_rows(partial_sum):
    return lax.psum_scatter(
        partial_sum.astype(jnp.bfloat16), "tensor", scatter_dimension=0, tiled=True
    ).astype(jnp.float32)


def scatter_weight(grad):
    return lax.psum_scatter(
        grad.astype(jnp.bfloat16), "dp", scatter_dimension=0, tiled=True
    ).astype(jnp.float32)


def on_device(
    tokens,
    lengths,
    dealing,
    project_weight,
    query_projection_bias,
    value_projection_bias,
    attention_output_weight,
    attention_output_bias,
    first_gain,
    first_shift,
    feed_input_weight,
    feed_input_bias,
    feed_output_weight,
    feed_output_bias,
    second_gain,
    second_shift,
    output_grad,
):
    n_data = lax.axis_size("dp")
    n_tensor = lax.axis_size("tensor")
    n_all = n_data * n_tensor
    data_index = lax.axis_index("dp")
    tensor_index = lax.axis_index("tensor")
    seq_total = dealing.shape[0]
    seq_here = seq_total // n_data
    piece_rows = tokens.shape[0]
    local_rows = piece_rows * n_data
    seq_rows = local_rows * n_tensor
    width = tokens.shape[2]
    head_cols = attention_output_weight.shape[1]
    heads_here = head_cols // HD
    hidden_cols = feed_input_weight.shape[1]
    score_scale = HD ** (-0.5)
    slot_ids = jnp.arange(seq_total, dtype=jnp.int32)
    placing = (dealing[None, :] == slot_ids[:, None]).astype(jnp.bfloat16)
    send_tokens = jnp.einsum(
        "qs,psd->pqd", placing, tokens, preferred_element_type=jnp.float32
    ).astype(jnp.bfloat16)
    send_grad = jnp.einsum(
        "qs,psd->pqd", placing, output_grad, preferred_element_type=jnp.float32
    ).astype(jnp.bfloat16)
    tokens_here = lax.all_to_all(send_tokens, "dp", split_axis=1, concat_axis=0, tiled=True)
    cotangent_here = lax.all_to_all(send_grad, "dp", split_axis=1, concat_axis=0, tiled=True)
    my_slots = data_index * seq_here + jnp.arange(seq_here, dtype=jnp.int32)
    mine = dealing[None, :] == my_slots[:, None]
    seq_length = jnp.sum(jnp.where(mine, lengths[None, :], 0), axis=1)
    row_ids = jnp.arange(seq_rows, dtype=jnp.int32)
    owner_rows = row_ids // local_rows
    inner_rows = row_ids % local_rows
    position = (
        inner_rows // piece_rows * n_tensor + owner_rows
    ) * piece_rows + inner_rows % piece_rows
    key_valid = position[None, :] < seq_length[:, None]
    project_full = lax.all_gather(project_weight, "dp", axis=0, tiled=True)
    output_full = lax.all_gather(attention_output_weight, "dp", axis=0, tiled=True)
    up_full = lax.all_gather(feed_input_weight, "dp", axis=0, tiled=True)
    down_full = lax.all_gather(feed_output_weight, "dp", axis=0, tiled=True)
    query_part = lax.dynamic_slice_in_dim(
        query_projection_bias, tensor_index * head_cols, head_cols
    )
    value_part = lax.dynamic_slice_in_dim(
        value_projection_bias, tensor_index * head_cols, head_cols
    )
    project_bias = jnp.concatenate([query_part, jnp.zeros_like(query_part), value_part])
    up_bias_here = lax.dynamic_slice_in_dim(
        feed_input_bias, tensor_index * hidden_cols, hidden_cols
    )

    def split_heads(qkv_block):
        query_rows = qkv_block[:, :head_cols].reshape(seq_rows, heads_here, HD)
        key_rows = qkv_block[:, head_cols : 2 * head_cols].reshape(seq_rows, heads_here, HD)
        value_rows = qkv_block[:, 2 * head_cols :].reshape(seq_rows, heads_here, HD)
        return (query_rows, key_rows, value_rows)

    def masked_scores(query_rows, key_rows, valid_keys):
        raw_scores = (
            jnp.einsum("qhe,khe->hqk", query_rows, key_rows, preferred_element_type=jnp.float32)
            * score_scale
        )
        return jnp.where(valid_keys[None, None, :], raw_scores, MASKED)

    def attend(qkv_block, valid_keys):
        query_rows, key_rows, value_rows = split_heads(qkv_block)
        scores = masked_scores(query_rows, key_rows, valid_keys)
        row_max = jnp.max(scores, axis=-1, keepdims=True)
        exponent = jnp.exp(scores - row_max)
        row_total = jnp.sum(exponent, axis=-1, keepdims=True)
        weights = (exponent / row_total).astype(jnp.bfloat16)
        mixed_heads = jnp.einsum(
            "hqk,khe->qhe", weights, value_rows, preferred_element_type=jnp.float32
        )
        return (
            mixed_heads.reshape(seq_rows, head_cols).astype(jnp.bfloat16),
            (row_max + jnp.log(row_total))[..., 0],
        )

    def attend_back(qkv_block, valid_keys, row_lse, grad_block):
        query_rows, key_rows, value_rows = split_heads(qkv_block)
        weights = jnp.exp(masked_scores(query_rows, key_rows, valid_keys) - row_lse[..., None])
        grad_heads = grad_block.reshape(seq_rows, heads_here, HD)
        grad_weights = jnp.einsum(
            "qhe,khe->hqk", grad_heads, value_rows, preferred_element_type=jnp.float32
        )
        inner_sum = jnp.sum(weights * grad_weights, axis=-1, keepdims=True)
        grad_scores = (weights * (grad_weights - inner_sum)).astype(jnp.bfloat16)
        grad_query = (
            jnp.einsum("hqk,khe->qhe", grad_scores, key_rows, preferred_element_type=jnp.float32)
            * score_scale
        )
        grad_key = (
            jnp.einsum("hqk,qhe->khe", grad_scores, query_rows, preferred_element_type=jnp.float32)
            * score_scale
        )
        grad_value = jnp.einsum(
            "hqk,qhe->khe",
            weights.astype(jnp.bfloat16),
            grad_heads,
            preferred_element_type=jnp.float32,
        )
        joined = jnp.concatenate(
            [
                grad_query.reshape(seq_rows, head_cols),
                grad_key.reshape(seq_rows, head_cols),
                grad_value.reshape(seq_rows, head_cols),
            ],
            axis=-1,
        )
        return joined.astype(jnp.bfloat16)

    gelu_exact = partial(jax.nn.gelu, approximate=False)
    seqs = range(seq_here)
    inputs_full = [gather_rows(tokens_here[:, s, :]) for s in seqs]
    projected = [
        (
            jnp.dot(inputs_full[s], project_full, preferred_element_type=jnp.float32) + project_bias
        ).astype(jnp.bfloat16)
        for s in seqs
    ]
    attended = [attend(projected[s], key_valid[s]) for s in seqs]
    mixed = [a[0] for a in attended]
    log_total = [a[1] for a in attended]
    branch = [
        scatter_rows(
            lax.dot_general(
                mixed[s], output_full, (((1,), (1,)), ((), ())), preferred_element_type=jnp.float32
            )
        )
        for s in seqs
    ]
    first = [
        norm_forward(
            tokens_here[:, s, :].astype(jnp.float32) + branch[s] + attention_output_bias,
            first_gain,
            first_shift,
        )
        for s in seqs
    ]
    first_full = [gather_rows(first[s][0].astype(jnp.bfloat16)) for s in seqs]
    preact = [
        jnp.dot(first_full[s], up_full, preferred_element_type=jnp.float32) + up_bias_here
        for s in seqs
    ]
    gelu_pairs = [jax.vjp(gelu_exact, preact[s]) for s in seqs]
    hidden = [g[0].astype(jnp.bfloat16) for g in gelu_pairs]
    feed = [
        scatter_rows(
            lax.dot_general(
                hidden[s], down_full, (((1,), (1,)), ((), ())), preferred_element_type=jnp.float32
            )
        )
        for s in seqs
    ]
    second = [
        norm_forward(first[s][0] + feed[s] + feed_output_bias, second_gain, second_shift)
        for s in seqs
    ]
    layer_output = jnp.stack([second[s][0] for s in seqs], axis=1).astype(jnp.bfloat16)
    cot = [cotangent_here[:, s, :].astype(jnp.float32) for s in seqs]
    second_gain_part = sum((jnp.sum(cot[s] * second[s][1], axis=0) for s in seqs))
    second_shift_part = sum((jnp.sum(cot[s], axis=0) for s in seqs))
    grad_second = [norm_backward(cot[s], second[s][1], second[s][2], second_gain) for s in seqs]
    down_bias_part = sum((jnp.sum(grad_second[s], axis=0) for s in seqs))
    grad_feed_full = [gather_rows(grad_second[s].astype(jnp.bfloat16)) for s in seqs]
    grad_hidden = [
        jnp.dot(grad_feed_full[s], down_full, preferred_element_type=jnp.float32) for s in seqs
    ]
    down_grad = sum(
        (
            lax.dot_general(
                grad_feed_full[s],
                hidden[s],
                (((0,), (0,)), ((), ())),
                preferred_element_type=jnp.float32,
            )
            for s in seqs
        )
    )
    down_shard = scatter_weight(down_grad)
    grad_preact = [gelu_pairs[s][1](grad_hidden[s])[0].astype(jnp.bfloat16) for s in seqs]
    up_grad = sum(
        (
            lax.dot_general(
                first_full[s],
                grad_preact[s],
                (((0,), (0,)), ((), ())),
                preferred_element_type=jnp.float32,
            )
            for s in seqs
        )
    )
    up_shard = scatter_weight(up_grad)
    up_bias_part = sum((jnp.sum(grad_preact[s], axis=0, dtype=jnp.float32) for s in seqs))
    grad_first = [
        grad_second[s]
        + scatter_rows(
            lax.dot_general(
                grad_preact[s],
                up_full,
                (((1,), (1,)), ((), ())),
                preferred_element_type=jnp.float32,
            )
        )
        for s in seqs
    ]
    first_gain_part = sum((jnp.sum(grad_first[s] * first[s][1], axis=0) for s in seqs))
    first_shift_part = sum((jnp.sum(grad_first[s], axis=0) for s in seqs))
    grad_residual = [
        norm_backward(grad_first[s], first[s][1], first[s][2], first_gain) for s in seqs
    ]
    output_bias_part = sum((jnp.sum(grad_residual[s], axis=0) for s in seqs))
    early_vectors = jnp.concatenate(
        [
            v.reshape(n_all, -1)
            for v in (
                output_bias_part,
                first_gain_part,
                first_shift_part,
                spread_block(up_bias_part, tensor_index, hidden_cols * n_tensor),
                down_bias_part,
                second_gain_part,
                second_shift_part,
            )
        ],
        axis=1,
    )
    early_reduced = lax.psum_scatter(
        early_vectors, ("dp", "tensor"), scatter_dimension=0, tiled=True
    )[0]
    branch_grad_full = [gather_rows(grad_residual[s].astype(jnp.bfloat16)) for s in seqs]
    grad_mixed = [
        jnp.dot(branch_grad_full[s], output_full, preferred_element_type=jnp.float32).astype(
            jnp.bfloat16
        )
        for s in seqs
    ]
    output_grad_weight = sum(
        (
            lax.dot_general(
                branch_grad_full[s],
                mixed[s],
                (((0,), (0,)), ((), ())),
                preferred_element_type=jnp.float32,
            )
            for s in seqs
        )
    )
    output_shard = scatter_weight(output_grad_weight)
    grad_projected = [
        attend_back(projected[s], key_valid[s], log_total[s], grad_mixed[s]) for s in seqs
    ]
    project_grad = sum(
        (
            lax.dot_general(
                inputs_full[s],
                grad_projected[s],
                (((0,), (0,)), ((), ())),
                preferred_element_type=jnp.float32,
            )
            for s in seqs
        )
    )
    project_shard = scatter_weight(project_grad)
    bias_sums = sum((jnp.sum(grad_projected[s], axis=0, dtype=jnp.float32) for s in seqs))
    late_vectors = jnp.concatenate(
        [
            spread_block(bias_sums[:head_cols], tensor_index, width).reshape(n_all, -1),
            spread_block(bias_sums[2 * head_cols :], tensor_index, width).reshape(n_all, -1),
        ],
        axis=1,
    )
    late_reduced = lax.psum_scatter(
        late_vectors, ("dp", "tensor"), scatter_dimension=0, tiled=True
    )[0]
    grad_inputs = [
        grad_residual[s]
        + scatter_rows(
            lax.dot_general(
                grad_projected[s],
                project_full,
                (((1,), (1,)), ((), ())),
                preferred_element_type=jnp.float32,
            )
        )
        for s in seqs
    ]
    grad_here = jnp.stack(grad_inputs, axis=1).astype(jnp.bfloat16)
    returned = lax.all_to_all(grad_here, "dp", split_axis=0, concat_axis=1, tiled=True)
    tokens_grad = jnp.einsum(
        "qs,pqd->psd", placing, returned, preferred_element_type=jnp.float32
    ).astype(jnp.bfloat16)
    vec_block = width // n_all
    early_split = [vec_block] * 3 + [hidden_cols * n_tensor // n_all] + [vec_block] * 3
    offsets = [sum(early_split[:k]) for k in range(len(early_split) + 1)]
    early = [early_reduced[offsets[k] : offsets[k + 1]] for k in range(len(early_split))]
    late = [late_reduced[:vec_block], late_reduced[vec_block:]]
    return (
        layer_output,
        tokens_grad,
        project_shard,
        late[0],
        late[1],
        output_shard,
        early[0],
        early[1],
        early[2],
        up_shard,
        early[3],
        down_shard,
        early[4],
        early[5],
        early[6],
    )


def solution(mesh):
    in_specs = (
        P(("dp", "tensor"), None, None),
        P(),
        P(),
        P("dp", "tensor"),
        P(),
        P(),
        P("dp", "tensor"),
        P(),
        P(),
        P(),
        P("dp", "tensor"),
        P(),
        P("dp", "tensor"),
        P(),
        P(),
        P(),
        P(("dp", "tensor"), None, None),
    )
    out_specs = (
        P("tensor", "dp", None),
        P(("dp", "tensor"), None, None),
        P("dp", "tensor"),
        P(("dp", "tensor")),
        P(("dp", "tensor")),
        P("dp", "tensor"),
        P(("dp", "tensor")),
        P(("dp", "tensor")),
        P(("dp", "tensor")),
        P("dp", "tensor"),
        P(("dp", "tensor")),
        P("dp", "tensor"),
        P(("dp", "tensor")),
        P(("dp", "tensor")),
        P(("dp", "tensor")),
    )
    return jax.shard_map(
        on_device, mesh=mesh, in_specs=in_specs, out_specs=out_specs, check_vma=False
    )
```

profile of v0, /device:TPU:0, one launch (start us, length us, event | category | flops | bytes accessed | tf_op | source)
XLA Modules:
  0.0 850.2 jit_solution(14724456239618128440)
XLA Ops:
  10.6 27.4 %all_to_all.54 = bf16[32,16,768]{2,0,1:T(8,128)(2,1)S(1)} all-to-all(bf16[32,16,768]{2,0,1:T(8,128)(2,1)S(1)} %copy.78), channel_id=1, replica_groups=mesh['dp'=8,'tensor'=4] {'dp'}, dimensions={1} | all-to-all | bytes 1572864 | tf_op jit(solution)/shard_map/all_to_all | solution.py:89
  41.7 31.2 %all_gather.38 = bf16[768,192]{1,0:T(8,128)(2,1)S(1)} all-gather(bf16[96,192]{1,0:T(8,128)(2,1)S(1)} %copy-done.49), channel_id=1, replica_groups=mesh['dp'=8,'tensor'=4] {'dp'}, dimensions={0}, use_global_device_ids=true | all-gather | bytes 331776 | tf_op jit(solution)/shard_map/all_gather | solution.py:102
  72.9 32.5 %all_gather.37 = bf16[768,576]{1,0:T(8,128)(2,1)S(1)} all-gather(bf16[96,576]{1,0:T(8,128)(2,1)S(1)} %copy-done.45), channel_id=1, replica_groups=mesh['dp'=8,'tensor'=4] {'dp'}, dimensions={0}, use_global_device_ids=true | all-gather | bytes 995328 | tf_op jit(solution)/shard_map/all_gather | solution.py:101
  109.1 3.2 add_convert_fusion.5
  116.6 2.8 copy-done.2
  128.4 3.1 copy-done.3
  136.4 14.9 %reduce-scatter.13.cloned.1.call-done = bf16[256,768]{1,0:T(8,128)(2,1)} async-done(((bf16[1024,768]{1,0:T(8,128)(2,1)}), bf16[256,768]{1,0:T(8,128)(2,1)}) %reduce-scatter.13.cloned.1.call-update) | async-done | bytes 393232 | tf_op jit(solution)/shard_map/reduce_scatter | solution.py:36
  152.6 29.1 %reduce-scatter.17.cloned.1.call-done = bf16[256,768]{1,0:T(8,128)(2,1)} async-done(((bf16[1024,768]{1,0:T(8,128)(2,1)}), bf16[256,768]{1,0:T(8,128)(2,1)}) %reduce-scatter.17.cloned.1.call-update) | async-done | bytes 393232 | tf_op jit(solution)/shard_map/reduce_scatter | solution.py:36
  189.2 17.3 %all-gather.19.cloned.1.call-done = bf16[1024,768]{1,0:T(8,128)(2,1)} async-done(((bf16[256,768]{1,0:T(8,128)(2,1)}), bf16[1024,768]{1,0:T(8,128)(2,1)}) %all-gather.19.cloned.1.call-update) | async-done | bytes 1572880 | tf_op jit(solution)/shard_map/all_gather | solution.py:32
  206.5 4.9 fusion.119
  211.4 16.7 %all-gather.13.cloned.1.call-done = bf16[1024,768]{1,0:T(8,128)(2,1)} async-done(((bf16[256,768]{1,0:T(8,128)(2,1)}), bf16[1024,768]{1,0:T(8,128)(2,1)}) %all-gather.13.cloned.1.call-update) | async-done | bytes 1572880 | tf_op jit(solution)/shard_map/all_gather | solution.py:32
  228.1 17.3 %multiply_convert_fusion.3 = (bf16[1024,768]{1,0:T(8,128)(2,1)}, f32[1024,768]{1,0:T(8,128)}, bf16[1024,768]{1,0:T(8,128)(2,1)}, f32[1024,768]{1,0:T(8,128)}, f32[1024,768]{1,0:T(8,128)}) fusion(f32[768]{0:T(1024)S(1)} %dynamic_slice.11, f32[1024,768]{1,0:T(8,128)} %fusion.119, bf16[1024,768]{1,0:T(8,128)(2,1)} %all-gather.13.cloned.1.call-done, ...), kind=kOutput, calls=%fused_computation.43 | convolution fusion | flops 1311768576 | bytes 18484224 | tf_op jit(solution)/shard_map/dot_general | solution.py:207
  245.4 26.3 %all-gather.17.cloned.1.call-done = bf16[768,768]{1,0:T(8,128)(2,1)} async-done(((bf16[96,768]{1,0:T(8,128)(2,1)}), bf16[768,768]{1,0:T(8,128)(2,1)}) %all-gather.17.cloned.1.call-update) | async-done | bytes 1179664 | tf_op jit(solution)/shard_map/all_gather | solution.py:104
  271.7 4.3 convolution_convert_fusion.6
  276.1 4.4 convolution_convert_fusion.4
  282.0 21.2 %all_to_all.55 = bf16[32,16,768]{2,0,1:T(8,128)(2,1)S(1)} all-to-all(bf16[32,16,768]{2,0,1:T(8,128)(2,1)S(1)} %copy.83), channel_id=1, replica_groups=mesh['dp'=8,'tensor'=4] {'dp'}, dimensions={1} | all-to-all | bytes 1572864 | tf_op jit(solution)/shard_map/all_to_all | solution.py:90
  303.4 29.6 %reduce-scatter.19.cloned.1.call-done = bf16[256,768]{1,0:T(8,128)(2,1)} async-done(((bf16[1024,768]{1,0:T(8,128)(2,1)}), bf16[256,768]{1,0:T(8,128)(2,1)}) %reduce-scatter.19.cloned.1.call-update) | async-done | bytes 393232 | tf_op jit(solution)/shard_map/reduce_scatter | solution.py:36
  336.7 3.2 fusion.108
  341.0 18.6 %all-gather.21.cloned.1.call-done = bf16[1024,768]{1,0:T(8,128)(2,1)} async-done(((bf16[256,768]{1,0:T(8,128)(2,1)}), bf16[1024,768]{1,0:T(8,128)(2,1)}) %all-gather.21.cloned.1.call-update) | async-done | bytes 1572880 | tf_op jit(solution)/shard_map/all_gather | solution.py:32
  359.7 4.8 fusion.120
  364.4 16.3 %all-gather.25.cloned.1.call-done = bf16[1024,768]{1,0:T(8,128)(2,1)} async-done(((bf16[256,768]{1,0:T(8,128)(2,1)}), bf16[1024,768]{1,0:T(8,128)(2,1)}) %all-gather.25.cloned.1.call-update) | async-done | bytes 1572880 | tf_op jit(solution)/shard_map/all_gather | solution.py:32
  380.8 11.5 %convert_reduce_fusion = (f32[768]{0:T(1024)}, bf16[1024,768]{1,0:T(8,128)(2,1)}, f32[768]{0:T(1024)}, bf16[1024,768]{1,0:T(8,128)(2,1)S(1)}) fusion(f32[1024,768]{1,0:T(8,128)} %get-tuple-element.152, f32[1024,768]{1,0:T(8,128)} %fusion.119, f32[768]{0:T(1024)} %copy-done.58, f32[1024,768]{1,0:T(8,128)} %fusion.120, f32[1024,768]{1,0:T(8,128)} %get-tuple-element.119, ...), kind=kOutput, calls=%fused_computation.26 | convolution fusion | flops 1234696704 | bytes 21636096 | tf_op jit(solution)/shard_map/dot_general | solution.py:232
  393.5 2.6 convolution_convert_fusion.3
  396.1 4.4 convolution_convert_fusion.2
  400.6 23.6 %reduce-scatter.21.cloned.1.call-done = bf16[256,768]{1,0:T(8,128)(2,1)} async-done(((bf16[1024,768]{1,0:T(8,128)(2,1)}), bf16[256,768]{1,0:T(8,128)(2,1)}) %reduce-scatter.21.cloned.1.call-update) | async-done | bytes 393232 | tf_op jit(solution)/shard_map/reduce_scatter | solution.py:36
  424.1 30.4 %reduce-scatter.25.cloned.1.call-done = bf16[256,768]{1,0:T(8,128)(2,1)} async-done(((bf16[1024,768]{1,0:T(8,128)(2,1)}), bf16[256,768]{1,0:T(8,128)(2,1)}) %reduce-scatter.25.cloned.1.call-update) | async-done | bytes 393232 | tf_op jit(solution)/shard_map/reduce_scatter | solution.py:36
  454.5 3.1 multiply_reduce_fusion.3
  457.7 2.9 fusion.107
  466.3 15.8 %all-gather.27.cloned.1.call-done = bf16[1024,768]{1,0:T(8,128)(2,1)} async-done(((bf16[256,768]{1,0:T(8,128)(2,1)}), bf16[1024,768]{1,0:T(8,128)(2,1)}) %all-gather.27.cloned.1.call-update) | async-done | bytes 1572880 | tf_op jit(solution)/shard_map/all_gather | solution.py:32
  484.3 6.1 multiply_reduce_fusion
  493.0 5.2 multiply_convert_fusion
  498.3 5.0 fusion.38
  506.6 2.6 convolution_convert_fusion
  511.7 6.4 multiply_reduce_fusion.1
  520.7 5.2 multiply_convert_fusion.1
  525.9 5.0 fusion.36
  534.3 2.6 convolution_convert_fusion.1
  537.0 3.5 fusion.123
  540.5 2.6 add_convert_fusion.2
  543.4 3.7 fusion.122
  557.2 3.2 fusion.24
  564.8 3.1 reduce-scatter.23.cloned.1.call-done
  571.8 5.5 all-to-all-start.2
  578.2 62.9 %reduce-scatter.35.cloned.1.call-done = bf16[96,768]{1,0:T(8,128)(2,1)} async-done(((bf16[768,768]{1,0:T(8,128)(2,1)}), bf16[96,768]{1,0:T(8,128)(2,1)}) %reduce-scatter.35.cloned.1.call-update) | async-done | bytes 147472 | tf_op jit(solution)/shard_map/reduce_scatter | solution.py:42
  642.7 65.5 %reduce-scatter.33.cloned.1.call-done = bf16[96,768]{1,0:T(8,128)(2,1)} async-done(((bf16[768,768]{1,0:T(8,128)(2,1)}), bf16[96,768]{1,0:T(8,128)(2,1)}) %reduce-scatter.33.cloned.1.call-update) | async-done | bytes 147472 | tf_op jit(solution)/shard_map/reduce_scatter | solution.py:42
  716.4 40.2 %all-reduce.2 = (f32[32,48]{1,0:T(8,128)S(1)}, f32[32,240]{1,0:T(8,128)S(1)}) all-reduce(f32[32,48]{1,0:T(8,128)S(1)} %pad_maximum_fusion.4, f32[32,240]{1,0:T(8,128)} %concatenate.21), channel_id=13, replica_groups=mesh['dp'=8,'tensor'=4] {'dp','tensor'}, use_global_device_ids=true, to_apply=%region_34.35.clone | all-reduce | flops 9216 | bytes 73728
  758.5 14.3 %reduce-scatter.31.cloned.1.call-done = bf16[96,192]{1,0:T(8,128)(2,1)} async-done(((bf16[768,192]{1,0:T(8,128)(2,1)}), bf16[96,192]{1,0:T(8,128)(2,1)}) %reduce-scatter.31.cloned.1.call-update) | async-done | bytes 36880 | tf_op jit(solution)/shard_map/reduce_scatter | solution.py:42
  774.2 64.8 %reduce-scatter.29.cloned.1.call-done = bf16[96,576]{1,0:T(8,128)(2,1)} async-done(((bf16[768,576]{1,0:T(8,128)(2,1)}), bf16[96,576]{1,0:T(8,128)(2,1)}) %reduce-scatter.29.cloned.1.call-update) | async-done | bytes 110608 | tf_op jit(solution)/shard_map/reduce_scatter | solution.py:42
  (309 shorter events, 102.2 us)
Async XLA Ops:
  8.0 97.4 %all-gather.31.cloned.1.call-start = ((), (), s32[]{:S(2)}) async-start(), calls=%async_computation.36 | async-start | bytes 1966080 | tf_op jit(solution)/shard_map/all_gather | solution.py:32
  10.5 30.9 %copy-start.56 = (s32[16]{0:T(128)S(1)}, s32[16]{0:T(128)}, u32[]{:S(2)}) copy-start(s32[16]{0:T(128)} %param.19) | copy-start | bytes 196
  10.5 30.9 %copy-start.59 = (s32[16]{0:T(128)S(1)}, s32[16]{0:T(128)}, u32[]{:S(2)}) copy-start(s32[16]{0:T(128)} %param.18) | copy-start | bytes 196
  10.6 31.2 %copy-start.49 = (bf16[96,192]{1,0:T(8,128)(2,1)S(1)}, bf16[96,192]{1,0:T(8,128)(2,1)}, u32[]{:S(2)}) copy-start(bf16[96,192]{1,0:T(8,128)(2,1)} %param.23) | copy-start | bytes 110596
  10.6 62.3 %copy-start.45 = (bf16[96,576]{1,0:T(8,128)(2,1)S(1)}, bf16[96,576]{1,0:T(8,128)(2,1)}, u32[]{:S(2)}) copy-start(bf16[96,576]{1,0:T(8,128)(2,1)} %param.20) | copy-start | bytes 331780
  39.0 70.1 %all-gather.29.cloned.1.call-start = ((), (), s32[]{:S(2)}) async-start(), calls=%async_computation.35 | async-start | bytes 1966080 | tf_op jit(solution)/shard_map/all_gather | solution.py:32
  39.7 111.6 %reduce-scatter.13.cloned.1.call-start = ((), (), s32[]{:S(2)}) async-start(), calls=%async_computation.15 | async-start | bytes 1966080 | tf_op jit(solution)/shard_map/reduce_scatter | solution.py:36
  109.0 15.2 %copy-start.17 = (bf16[1024,192]{0,1:T(8,128)(2,1)}, bf16[1024,192]{0,1:T(8,128)(2,1)S(1)}, u32[]{:S(2)}) copy-start(bf16[1024,192]{0,1:T(8,128)(2,1)S(1)} %get-tuple-element.127) | copy-start | bytes 1179652
  109.0 15.2 %copy-start.19 = (bf16[1024,192]{0,1:T(8,128)(2,1)}, bf16[1024,192]{0,1:T(8,128)(2,1)S(1)}, u32[]{:S(2)}) copy-start(bf16[1024,192]{0,1:T(8,128)(2,1)S(1)} %get-tuple-element.128) | copy-start | bytes 1179652
  109.0 19.4 %copy-start.23 = (bf16[1024,192]{0,1:T(8,128)(2,1)}, bf16[1024,192]{0,1:T(8,128)(2,1)S(1)}, u32[]{:S(2)}) copy-start(bf16[1024,192]{0,1:T(8,128)(2,1)S(1)} %get-tuple-element.129) | copy-start | bytes 1179652
  123.7 58.0 %reduce-scatter.17.cloned.1.call-start = ((), (), s32[]{:S(2)}) async-start(), calls=%async_computation.20 | async-start | bytes 1966080 | tf_op jit(solution)/shard_map/reduce_scatter | solution.py:36
  133.9 49.3 %copy-start.25 = (bf16[3,64,1024]{2,1,0:T(8,128)(2,1)}, bf16[3,64,1024]{2,1,0:T(8,128)(2,1)S(1)}, u32[]{:S(2)}) copy-start(bf16[3,64,1024]{2,1,0:T(8,128)(2,1)S(1)} %fusion.46) | copy-start | bytes 1179652
  133.9 17.4 %copy-start.42 = (f32[768]{0:T(1024)S(1)}, f32[768]{0:T(1024)}, u32[]{:S(2)}) copy-start(f32[768]{0:T(1024)} %param.24) | copy-start | bytes 9220
  133.9 50.6 %copy-start.48 = (f32[768]{0:T(1024)S(1)}, f32[768]{0:T(1024)}, u32[]{:S(2)}) copy-start(f32[768]{0:T(1024)} %param.25) | copy-start | bytes 9220
  133.9 50.6 %copy-start.54 = (f32[768]{0:T(1024)S(1)}, f32[768]{0:T(1024)}, u32[]{:S(2)}) copy-start(f32[768]{0:T(1024)} %param.26) | copy-start | bytes 9220
  135.7 53.5 %all-gather.15.cloned.1.call-start = ((), (), s32[]{:S(2)}) async-start(), calls=%async_computation.17 | async-start | bytes 1327104 | tf_op jit(solution)/shard_map/all_gather | solution.py:103
  136.3 70.2 %all-gather.19.cloned.1.call-start = ((), (), s32[]{:S(2)}) async-start(), calls=%async_computation.21 | async-start | bytes 1966080 | tf_op jit(solution)/shard_map/all_gather | solution.py:32
  151.3 33.2 %copy-start.6 = (bf16[256,768]{1,0:T(8,128)(2,1)S(1)}, bf16[256,768]{1,0:T(8,128)(2,1)}, u32[]{:S(2)}) copy-start(bf16[256,768]{1,0:T(8,128)(2,1)} %reduce-scatter.13.cloned.1.call-done) | copy-start | bytes 1179652
  183.2 28.1 %copy-start.51 = (f32[256]{0:T(256)}, f32[256]{0:T(256)S(1)}, u32[]{:S(2)}) copy-start(f32[256]{0:T(256)S(1)} %get-tuple-element.164) | copy-start | bytes 3076
  184.5 26.9 %copy-start.50 = (f32[256]{0:T(256)}, f32[256]{0:T(256)S(1)}, u32[]{:S(2)}) copy-start(f32[256]{0:T(256)S(1)} %add_rsqrt_fusion.1) | copy-start | bytes 3076
  186.9 41.2 %all-gather.13.cloned.1.call-start = ((), (), s32[]{:S(2)}) async-start(), calls=%async_computation.16 | async-start | bytes 1966080 | tf_op jit(solution)/shard_map/all_gather | solution.py:32
  187.5 84.2 %all-gather.17.cloned.1.call-start = ((), (), s32[]{:S(2)}) async-start(), calls=%async_computation.18 | async-start | bytes 1327104 | tf_op jit(solution)/shard_map/all_gather | solution.py:104
  188.2 115.2 %reduce-scatter.15.cloned.1.call-start = ((), (), s32[]{:S(2)}) async-start(), calls=%async_computation.19 | async-start | bytes 1966080 | tf_op jit(solution)/shard_map/reduce_scatter | solution.py:36
  189.2 38.8 %copy-start.58 = (f32[768]{0:T(1024)}, f32[768]{0:T(1024)S(1)}, u32[]{:S(2)}) copy-start(f32[768]{0:T(1024)S(1)} %dynamic_slice.11) | copy-start | bytes 9220
  189.2 38.8 %copy-start.63 = (bf16[768,768]{1,0:T(8,128)(2,1)S(1)}, bf16[768,768]{1,0:T(8,128)(2,1)}, u32[]{:S(2)}) copy-start(bf16[768,768]{1,0:T(8,128)(2,1)} %all-gather.15.cloned.1.call-done) | copy-start | bytes 3538948
  276.0 57.0 %reduce-scatter.19.cloned.1.call-start = ((), (), s32[]{:S(2)}) async-start(), calls=%async_computation.22 | async-start | bytes 1966080 | tf_op jit(solution)/shard_map/reduce_scatter | solution.py:36
  280.5 52.5 %copy-start.7 = (bf16[256,768]{1,0:T(8,128)(2,1)S(1)}, bf16[256,768]{1,0:T(8,128)(2,1)}, u32[]{:S(2)}) copy-start(bf16[256,768]{1,0:T(8,128)(2,1)} %reduce-scatter.17.cloned.1.call-done) | copy-start | bytes 1179652
  280.5 79.1 %all-gather.21.cloned.1.call-start = ((), (), s32[]{:S(2)}) async-start(), calls=%async_computation.23 | async-start | bytes 1966080 | tf_op jit(solution)/shard_map/all_gather | solution.py:32
  303.3 32.1 %copy-start.55 = (f32[768]{0:T(1024)S(1)}, f32[768]{0:T(1024)}, u32[]{:S(2)}) copy-start(f32[768]{0:T(1024)} %param.31) | copy-start | bytes 9220
  339.9 40.9 %all-gather.25.cloned.1.call-start = ((), (), s32[]{:S(2)}) async-start(), calls=%async_computation.27 | async-start | bytes 1966080 | tf_op jit(solution)/shard_map/all_gather | solution.py:32
  340.8 83.4 %reduce-scatter.21.cloned.1.call-start = ((), (), s32[]{:S(2)}) async-start(), calls=%async_computation.24 | async-start | bytes 1966080 | tf_op jit(solution)/shard_map/reduce_scatter | solution.py:36
  380.8 12.7 %copy-start.64 = (bf16[768,768]{1,0:T(8,128)(2,1)S(1)}, bf16[768,768]{1,0:T(8,128)(2,1)}, u32[]{:S(2)}) copy-start(bf16[768,768]{1,0:T(8,128)(2,1)} %all-gather.15.cloned.1.call-done) | copy-start | bytes 3538948
  396.1 58.5 %reduce-scatter.25.cloned.1.call-start = ((), (), s32[]{:S(2)}) async-start(), calls=%async_computation.28 | async-start | bytes 1966080 | tf_op jit(solution)/shard_map/reduce_scatter | solution.py:36
  400.5 81.6 %all-gather.27.cloned.1.call-start = ((), (), s32[]{:S(2)}) async-start(), calls=%async_computation.29 | async-start | bytes 1966080 | tf_op jit(solution)/shard_map/all_gather | solution.py:32
  460.6 23.6 %copy-start.24 = (bf16[1024,192]{0,1:T(8,128)(2,1)S(1)}, bf16[1024,192]{0,1:T(8,128)(2,1)}, u32[]{:S(2)}) copy-start(bf16[1024,192]{0,1:T(8,128)(2,1)} %copy-done.23) | copy-start | bytes 1179652
  462.4 47.2 %all-gather.23.cloned.1.call-start = ((), (), s32[]{:S(2)}) async-start(), calls=%async_computation.25 | async-start | bytes 1966080 | tf_op jit(solution)/shard_map/all_gather | solution.py:32
  465.8 97.0 %reduce-scatter.27.cloned.1.call-start = ((), (), s32[]{:S(2)}) async-start(), calls=%async_computation.30 | async-start | bytes 1966080 | tf_op jit(solution)/shard_map/reduce_scatter | solution.py:36
  509.3 58.6 %reduce-scatter.23.cloned.1.call-start = ((), (), s32[]{:S(2)}) async-start(), calls=%async_computation.26 | async-start | bytes 1966080 | tf_op jit(solution)/shard_map/reduce_scatter | solution.py:36
  511.7 9.1 %slice-start.2 = ((s8[12582912]{0:T(1024)(128)(4,1)}), s8[4194304]{0:T(1024)(128)(4,1)S(1)}, s32[]{:S(2)}) async-start(s8[12582912]{0:T(1024)(128)(4,1)} %bitcast.234), calls=%async_computation.39 | async-start | bytes 8388608
  536.9 104.2 %reduce-scatter.35.cloned.1.call-start = ((), (), s32[]{:S(2)}) async-start(), calls=%async_computation.34 | async-start | bytes 1327104 | tf_op jit(solution)/shard_map/reduce_scatter | solution.py:42
  543.1 165.1 %reduce-scatter.33.cloned.1.call-start = ((), (), s32[]{:S(2)}) async-start(), calls=%async_computation.33 | async-start | bytes 1327104 | tf_op jit(solution)/shard_map/reduce_scatter | solution.py:42
  549.7 223.0 %reduce-scatter.31.cloned.1.call-start = ((), (), s32[]{:S(2)}) async-start(), calls=%async_computation.32 | async-start | bytes 442368 | tf_op jit(solution)/shard_map/reduce_scatter | solution.py:42
  557.2 281.9 %reduce-scatter.29.cloned.1.call-start = ((), (), s32[]{:S(2)}) async-start(), calls=%async_computation.31 | async-start | bytes 1105920 | tf_op jit(solution)/shard_map/reduce_scatter | solution.py:42
  568.9 145.5 %copy-start.28 = (bf16[3,64,1024]{2,1,0:T(8,128)(2,1)S(1)}, bf16[3,64,1024]{2,1,0:T(8,128)(2,1)}, u32[]{:S(2)}) copy-start(bf16[3,64,1024]{2,1,0:T(8,128)(2,1)} %copy-done.27) | copy-start | bytes 1179652
  568.9 145.5 %copy-start.30 = (bf16[3,64,1024]{2,1,0:T(8,128)(2,1)S(1)}, bf16[3,64,1024]{2,1,0:T(8,128)(2,1)}, u32[]{:S(2)}) copy-start(bf16[3,64,1024]{2,1,0:T(8,128)(2,1)} %copy-done.29) | copy-start | bytes 1179652
  571.8 268.9 %all-to-all-start.2 = ((bf16[256,2,768]{2,1,0:T(2,128)(2,1)}), bf16[256,2,768]{2,1,0:T(2,128)(2,1)S(1)}, u32[]{:S(2)}, u32[]{:S(2)}) async-start(bf16[256,2,768]{2,1,0:T(2,128)(2,1)} %copy.91), calls=%async_computation.10 | async-start | bytes 1572864 | tf_op jit(solution)/shard_map/all_to_all | solution.py:354
  714.4 127.1 %copy-start.57 = (s32[16]{0:T(128)S(1)}, s32[16]{0:T(128)}, u32[]{:S(2)}) copy-start(s32[16]{0:T(128)} %param.19) | copy-start | bytes 196
  714.4 128.4 %copy-start.1 = (bf16[32,16,768]{2,1,0:T(8,128)(2,1)S(1)}, bf16[32,16,768]{2,1,0:T(8,128)(2,1)}, u32[]{:S(2)}) copy-start(bf16[32,16,768]{2,1,0:T(8,128)(2,1)} %param.17) | copy-start | bytes 2359300
  (49 other events, 197.6 us)
Sparse Core Ops, SparseCore 0:
  39.1 18.6 all-gather.30
  59.9 19.6 all-gather.28
  123.8 27.3 reduce-scatter.12
  153.7 27.9 reduce-scatter.16
  340.0 19.6 all-gather.20
  361.1 19.6 all-gather.24
  462.5 19.6 all-gather.26
  483.7 19.6 all-gather.22
  509.4 27.9 reduce-scatter.26
  539.8 27.9 reduce-scatter.22
  571.2 69.7 reduce-scatter.34
  644.3 63.8 reduce-scatter.32
  711.5 61.2 reduce-scatter.30
  776.0 63.0 reduce-scatter.28
Sparse Core Ops, SparseCore 1:
  138.4 40.5 all-gather.14
  187.0 19.5 all-gather.18
  208.5 19.5 all-gather.12
  230.3 41.4 all-gather.16
  276.1 26.3 reduce-scatter.14
  305.0 27.9 reduce-scatter.18
  396.2 27.9 reduce-scatter.20
  426.6 27.9 reduce-scatter.24
where the time goes:
time: 859 us; the launch traced here: 850 us
  waiting for transfers between devices  452 us (53%)
  blocking collectives  153 us (18%)
  matrix products  136 us (16%)
  other arithmetic  55.4 us (6%)
  local copies, waits for them, and re-layouts  28.8 us (3%)
  between operations  16.9 us (2%)
    reduce_scatter x4, waiting for transfers between devices, scatter_weight(): lax.psum_scatter(grad.astype(jnp.bfloat16), 'dp', scatter_dimension=0, ti...  208 us
    reduce_scatter x8, waiting for transfers between devices, scatter_rows(): lax.psum_scatter(partial_sum.astype(jnp.bfloat16), 'tensor', scatter_dime...  131 us
    all_gather x8, waiting for transfers between devices, gather_rows(): return lax.all_gather(block, 'tensor', axis=0, tiled=True)  84.8 us
    unnamed x1, blocking collectives  40.2 us
    all_gather x1, blocking collectives, on_device(): project_full = lax.all_gather(project_weight, 'dp', axis=0, tiled=True)  32.5 us
    all_gather x1, blocking collectives, on_device(): lax.all_gather(attention_output_weight, 'dp', axis=0, tiled=True)  31.2 us
    all_to_all x1, blocking collectives, on_device(): lax.all_to_all(send_tokens, 'dp', split_axis=1, concat_axis=0, tiled=True)  27.4 us
    all_gather x1, waiting for transfers between devices, on_device(): down_full = lax.all_gather(feed_output_weight, 'dp', axis=0, tiled=True)  26.3 us
  transfers between devices with their start and end apart: 23, of which 16 were waited for; matrix products, arithmetic and copies ran while one was open for 18% of the time, Pallas kernels for 0%

commit v1 on v0

--- a/solution.py
+++ b/solution.py
@@ -9,6 +9,22 @@
 MASKED = -1e30
 
 
+def ring_gather(x, axis, dim):
+    ways, here, step = (lax.axis_size(axis), lax.axis_index(axis), x.shape[dim])
+    shape = [n * ways if d == dim else n for d, n in enumerate(x.shape)]
+    full = lax.dynamic_update_slice_in_dim(jnp.zeros(shape, x.dtype), x, here * step, axis=dim)
+    going_up = going_down = x
+    for far in range(1, ways // 2 + 1):
+        going_up = lax.ppermute(going_up, axis, [(d, (d + 1) % ways) for d in range(ways)])
+        full = lax.dynamic_update_slice_in_dim(full, going_up, (here - far) % ways * step, axis=dim)
+        if 2 * far < ways:
+            going_down = lax.ppermute(going_down, axis, [(d, (d - 1) % ways) for d in range(ways)])
+            full = lax.dynamic_update_slice_in_dim(
+                full, going_down, (here + far) % ways * step, axis=dim
+            )
+    return full
+
+
 def norm_forward(value, gain, shift):
     centred = value - jnp.mean(value, axis=-1, keepdims=True)
     inverse = lax.rsqrt(jnp.mean(centred * centred, axis=-1, keepdims=True) + EPSILON)
@@ -29,7 +45,7 @@
 
 
 def gather_rows(block):
-    return lax.all_gather(block, "tensor", axis=0, tiled=True)
+    return ring_gather(block, "tensor", 0)
 
 
 def scatter_rows(partial_sum):

time: 859 us -> 823 us (0.958)
  waiting for transfers between devices: 452 us -> 422 us
  starting transfers between devices: 8.07 us -> 25.1 us
  matrix products: 136 us -> 120 us
  local copies, waits for them, and re-layouts: 28.8 us -> 44 us
  blocking collectives: 153 us -> 140 us
  other arithmetic: 55.4 us -> 45.9 us
    all_gather x8 -> x0, waiting for transfers between devices: 84.8 us -> none  [gather_rows(): return lax.all_gather(block, 'tensor', axis=0, tiled=True)]
    ppermute x0 -> x24, waiting for transfers between devices: none -> 80.8 us  [the longest x16 72.6 us: ring_gather(): lax.ppermute(going_up, axis, [(d, (d + 1) % ways) for d in range(ways)])]
    all_to_all x1 -> x0, blocking collectives: 27.4 us -> none  [on_device(): lax.all_to_all(send_tokens, 'dp', split_axis=1, concat_axis=0, tiled=True)]
    all_gather x1, waiting for transfers between devices: 26.3 us -> 0.01 us  [on_device(): down_full = lax.all_gather(feed_output_weight, 'dp', axis=0, tiled=True)]
    ppermute x0 -> x24, starting transfers between devices: none -> 10.7 us  [the longest x8 8.91 us: ring_gather(): lax.ppermute(going_down, axis, [(d, (d - 1) % ways) for d in range(ways)])]
    all_gather x1, blocking collectives: 31.2 us -> 40.7 us  [on_device(): lax.all_gather(attention_output_weight, 'dp', axis=0, tiled=True)]
    dynamic_update_slice x0 -> x26, local copies, waits for them, and re-layouts: none -> 9.35 us  [the longest x16 6.31 us: ring_gather(): lax.dynamic_update_slice_in_dim(full, going_up, (here - far) % ways * ste...]
    dot_general x2, matrix products: 16.3 us -> 7.32 us  [on_device(): jnp.dot(grad_feed_full[s], down_full, preferred_element_type=jnp.float32)]
  transfers between devices with their start and end apart: 23 -> 40, of which waited for: 16 -> 26; matrix products, arithmetic and copies ran while one was open for 18% -> 19% of each run, Pallas kernels for 0% -> 0%
where the time goes in v1:
time: 823 us; the launch traced here: 815 us
  waiting for transfers between devices  422 us (51%)
  blocking collectives  140 us (17%)
  matrix products  120 us (15%)
  other arithmetic  45.9 us (6%)
  local copies, waits for them, and re-layouts  44 us (5%)
  starting transfers between devices  25.1 us (3%)
  between operations  17.9 us (2%)
    reduce_scatter x4, waiting for transfers between devices, scatter_weight(): lax.psum_scatter(grad.astype(jnp.bfloat16), 'dp', scatter_dimension=0, ti...  212 us
    reduce_scatter x8, waiting for transfers between devices, scatter_rows(): lax.psum_scatter(partial_sum.astype(jnp.bfloat16), 'tensor', scatter_dime...  128 us
    ppermute x16, waiting for transfers between devices, ring_gather(): lax.ppermute(going_up, axis, [(d, (d + 1) % ways) for d in range(ways)])  72.6 us
    all_gather x1, blocking collectives, on_device(): lax.all_gather(attention_output_weight, 'dp', axis=0, tiled=True)  40.7 us
    unnamed x1, blocking collectives  40.2 us
    all_gather x1, blocking collectives, on_device(): project_full = lax.all_gather(project_weight, 'dp', axis=0, tiled=True)  34.9 us
    all_to_all x1, blocking collectives, on_device(): lax.all_to_all(send_grad, 'dp', split_axis=1, concat_axis=0, tiled=True)  23.7 us
    unnamed x224, local copies, waits for them, and re-layouts  22.7 us
  transfers between devices with their start and end apart: 40, of which 26 were waited for; matrix products, arithmetic and copies ran while one was open for 19% of the time, Pallas kernels for 0%

profile of v1, /device:TPU:0, one launch (start us, length us, event | category | flops | bytes accessed | tf_op | source)
XLA Modules:
  0.0 814.5 jit_solution(14738290767401045499)
XLA Ops:
  11.4 7.3 all-to-all-start
  20.8 40.7 %all_gather.13 = bf16[768,192]{1,0:T(8,128)(2,1)S(1)} all-gather(bf16[96,192]{1,0:T(8,128)(2,1)S(1)} %copy-done.67), channel_id=1, replica_groups=mesh['dp'=8,'tensor'=4] {'dp'}, dimensions={0}, use_global_device_ids=true | all-gather | bytes 331776 | tf_op jit(solution)/shard_map/all_gather | solution.py:118
  61.5 34.9 %all_gather.12 = bf16[768,576]{1,0:T(8,128)(2,1)} all-gather(bf16[96,576]{1,0:T(8,128)(2,1)S(1)} %copy-done.60), channel_id=1, replica_groups=mesh['dp'=8,'tensor'=4] {'dp'}, dimensions={0}, use_global_device_ids=true | all-gather | bytes 995328 | tf_op jit(solution)/shard_map/all_gather | solution.py:117
  100.4 5.9 collective-permute-done
  106.2 8.4 %collective-permute-done.6 = bf16[256,768]{1,0:T(8,128)(2,1)S(1)} collective-permute-done((bf16[256,768]{1,0:T(8,128)(2,1)S(1)}, bf16[256,768]{1,0:T(8,128)(2,1)S(1)}, u32[]{:S(2)}, u32[]{:S(2)}) %collective-permute-start.6) | collective-permute-done | bytes 393248 | tf_op jit(solution)/shard_map/ppermute | solution.py:18
  116.3 4.3 collective-permute-done.2
  126.1 2.9 copy-done.3
  134.5 2.9 add_convert_fusion.4
  141.7 2.9 copy-done.2
  150.2 9.1 %reduce-scatter.13.cloned.1.call-done = bf16[256,768]{1,0:T(8,128)(2,1)} async-done(((bf16[1024,768]{1,0:T(8,128)(2,1)}), bf16[256,768]{1,0:T(8,128)(2,1)}) %reduce-scatter.13.cloned.1.call-update) | async-done | bytes 393232 | tf_op jit(solution)/shard_map/reduce_scatter | solution.py:52
  160.6 29.3 %reduce-scatter.17.cloned.1.call-done = bf16[256,768]{1,0:T(8,128)(2,1)} async-done(((bf16[1024,768]{1,0:T(8,128)(2,1)}), bf16[256,768]{1,0:T(8,128)(2,1)}) %reduce-scatter.17.cloned.1.call-update) | async-done | bytes 393232 | tf_op jit(solution)/shard_map/reduce_scatter | solution.py:52
  202.7 7.4 collective-permute-done.9
  213.1 3.0 collective-permute-done.10
  217.9 3.9 collective-permute-done.11
  222.6 3.4 fusion.110
  227.6 17.3 %multiply_convert_fusion.3 = (bf16[1024,768]{1,0:T(8,128)(2,1)}, f32[1024,768]{1,0:T(8,128)}, bf16[1024,768]{1,0:T(8,128)(2,1)}, f32[1024,768]{1,0:T(8,128)}, f32[1024,768]{1,0:T(8,128)}) fusion(f32[768]{0:T(1024)S(1)} %dynamic_slice.11, f32[1024,768]{1,0:T(8,128)S(1)} %fusion.110, bf16[1024,768]{1,0:T(8,128)(2,1)S(1)} %constant_dynamic-update-slice_fusion.24, ...), kind=kOutput, calls=%fused_computation.43 | convolution fusion | flops 1311768576 | bytes 18484224 | tf_op jit(solution)/shard_map/dot_general | solution.py:223
  245.0 4.3 convolution_convert_fusion.6
  249.4 4.4 convolution_convert_fusion.4
  254.6 23.7 %all_to_all.54 = bf16[32,16,768]{2,0,1:T(8,128)(2,1)S(1)} all-to-all(bf16[32,16,768]{2,0,1:T(8,128)(2,1)S(1)} %copy.83), channel_id=1, replica_groups=mesh['dp'=8,'tensor'=4] {'dp'}, dimensions={1} | all-to-all | bytes 1572864 | tf_op jit(solution)/shard_map/all_to_all | solution.py:106
  278.4 29.6 %reduce-scatter.19.cloned.1.call-done = bf16[256,768]{1,0:T(8,128)(2,1)} async-done(((bf16[1024,768]{1,0:T(8,128)(2,1)}), bf16[256,768]{1,0:T(8,128)(2,1)}) %reduce-scatter.19.cloned.1.call-update) | async-done | bytes 393232 | tf_op jit(solution)/shard_map/reduce_scatter | solution.py:52
  317.9 5.9 collective-permute-done.18
  323.8 8.4 %collective-permute-done.12 = bf16[256,768]{1,0:T(8,128)(2,1)S(1)} collective-permute-done((bf16[256,768]{1,0:T(8,128)(2,1)S(1)}, bf16[256,768]{1,0:T(8,128)(2,1)S(1)}, u32[]{:S(2)}, u32[]{:S(2)}) %collective-permute-start.12) | collective-permute-done | bytes 393248 | tf_op jit(solution)/shard_map/ppermute | solution.py:18
  332.6 2.8 collective-permute-done.13
  335.4 7.2 collective-permute-done.14
  347.6 5.9 convert_reduce_fusion
  357.4 4.3 convolution_convert_fusion.3
  361.8 23.7 %reduce-scatter.25.cloned.1.call-done = bf16[256,768]{1,0:T(8,128)(2,1)} async-done(((bf16[1024,768]{1,0:T(8,128)(2,1)}), bf16[256,768]{1,0:T(8,128)(2,1)}) %reduce-scatter.25.cloned.1.call-update) | async-done | bytes 393232 | tf_op jit(solution)/shard_map/reduce_scatter | solution.py:52
  385.5 30.4 %reduce-scatter.21.cloned.1.call-done = bf16[256,768]{1,0:T(8,128)(2,1)} async-done(((bf16[1024,768]{1,0:T(8,128)(2,1)}), bf16[256,768]{1,0:T(8,128)(2,1)}) %reduce-scatter.21.cloned.1.call-update) | async-done | bytes 393232 | tf_op jit(solution)/shard_map/reduce_scatter | solution.py:52
  415.9 3.1 multiply_reduce_fusion.3
  424.2 6.8 collective-permute-done.15
  431.1 8.5 %collective-permute-done.21 = bf16[256,768]{1,0:T(8,128)(2,1)} collective-permute-done((bf16[256,768]{1,0:T(8,128)(2,1)S(1)}, bf16[256,768]{1,0:T(8,128)(2,1)}, u32[]{:S(2)}, u32[]{:S(2)}) %collective-permute-start.21) | collective-permute-done | bytes 393248 | tf_op jit(solution)/shard_map/ppermute | solution.py:18
  442.1 3.3 collective-permute-done.17
  446.6 6.1 multiply_reduce_fusion.1
  456.5 5.2 multiply_convert_fusion.1
  461.7 4.1 fusion.27
  473.3 6.1 multiply_reduce_fusion
  482.3 5.3 multiply_convert_fusion
  487.5 4.4 fusion.29
  499.3 3.5 fusion.114
  505.7 3.5 fusion.113
  518.9 3.1 fusion.94
  526.3 5.5 reduce-scatter.27.cloned.1.call-done
  535.8 5.7 all-to-all-start.2
  542.3 63.0 %reduce-scatter.35.cloned.1.call-done = bf16[96,768]{1,0:T(8,128)(2,1)} async-done(((bf16[768,768]{1,0:T(8,128)(2,1)}), bf16[96,768]{1,0:T(8,128)(2,1)}) %reduce-scatter.35.cloned.1.call-update) | async-done | bytes 147472 | tf_op jit(solution)/shard_map/reduce_scatter | solution.py:58
  606.9 65.4 %reduce-scatter.33.cloned.1.call-done = bf16[96,768]{1,0:T(8,128)(2,1)} async-done(((bf16[768,768]{1,0:T(8,128)(2,1)}), bf16[96,768]{1,0:T(8,128)(2,1)}) %reduce-scatter.33.cloned.1.call-update) | async-done | bytes 147472 | tf_op jit(solution)/shard_map/reduce_scatter | solution.py:58
  675.6 40.2 %all-reduce.2 = (f32[32,48]{1,0:T(8,128)S(1)}, f32[32,240]{1,0:T(8,128)S(1)}) all-reduce(f32[32,48]{1,0:T(8,128)S(1)} %pad_maximum_fusion.4, f32[32,240]{1,0:T(8,128)S(1)} %concatenate.21), channel_id=11, replica_groups=mesh['dp'=8,'tensor'=4] {'dp','tensor'}, use_global_device_ids=true, to_apply=%region_34.35.clone | all-reduce | flops 9216 | bytes 73728
  717.5 19.2 %reduce-scatter.31.cloned.1.call-done = bf16[96,192]{1,0:T(8,128)(2,1)} async-done(((bf16[768,192]{1,0:T(8,128)(2,1)}), bf16[96,192]{1,0:T(8,128)(2,1)}) %reduce-scatter.31.cloned.1.call-update) | async-done | bytes 36880 | tf_op jit(solution)/shard_map/reduce_scatter | solution.py:58
  738.2 64.9 %reduce-scatter.29.cloned.1.call-done = bf16[96,576]{1,0:T(8,128)(2,1)} async-done(((bf16[768,576]{1,0:T(8,128)(2,1)}), bf16[96,576]{1,0:T(8,128)(2,1)}) %reduce-scatter.29.cloned.1.call-update) | async-done | bytes 110608 | tf_op jit(solution)/shard_map/reduce_scatter | solution.py:58
  (444 shorter events, 135.4 us)
Async XLA Ops:
  11.4 85.0 %all-to-all-start = ((bf16[32,16,768]{2,0,1:T(8,128)(2,1)}), bf16[32,16,768]{2,0,1:T(8,128)(2,1)S(1)}, u32[]{:S(2)}, u32[]{:S(2)}) async-start(bf16[32,16,768]{2,0,1:T(8,128)(2,1)} %copy.78), calls=%async_computation | async-start | bytes 1572864 | tf_op jit(solution)/shard_map/all_to_all | solution.py:105
  18.7 140.6 %reduce-scatter.13.cloned.1.call-start = ((), (), s32[]{:S(2)}) async-start(), calls=%async_computation.15 | async-start | bytes 1966080 | tf_op jit(solution)/shard_map/reduce_scatter | solution.py:52
  96.5 9.7 %collective-permute-start = (bf16[256,768]{1,0:T(8,128)(2,1)S(1)}, bf16[256,768]{1,0:T(8,128)(2,1)S(1)}, u32[]{:S(2)}, u32[]{:S(2)}) collective-permute-start(bf16[256,768]{1,0:T(8,128)(2,1)S(1)} %get-tuple-element.147), channel_id=1, source_target_pairs={{0,1},{1,2},{2,3},{3,0},{4,5},{5,6},{6,7},{7,4},{8,9},{9,10},{10,1... | collective-permute-start | bytes 1179656 | tf_op jit(solution)/shard_map/ppermute | solution.py:18
  96.6 18.2 %collective-permute-start.1 = (bf16[256,768]{1,0:T(8,128)(2,1)S(1)}, bf16[256,768]{1,0:T(8,128)(2,1)S(1)}, u32[]{:S(2)}, u32[]{:S(2)}) collective-permute-start(bf16[256,768]{1,0:T(8,128)(2,1)S(1)} %get-tuple-element.147), channel_id=1, source_target_pairs={{0,3},{1,0},{2,1},{3,2},{4,7},{5,4},{6,5},{7,6},{8,11},{9,8},{10,9... | collective-permute-start | bytes 1179656 | tf_op jit(solution)/shard_map/ppermute | solution.py:21
  98.3 16.4 %collective-permute-start.6 = (bf16[256,768]{1,0:T(8,128)(2,1)S(1)}, bf16[256,768]{1,0:T(8,128)(2,1)S(1)}, u32[]{:S(2)}, u32[]{:S(2)}) collective-permute-start(bf16[256,768]{1,0:T(8,128)(2,1)S(1)} %get-tuple-element.148), channel_id=1, source_target_pairs={{0,1},{1,2},{2,3},{3,0},{4,5},{5,6},{6,7},{7,4},{8,9},{9,10},{10,1... | collective-permute-start | bytes 1179656 | tf_op jit(solution)/shard_map/ppermute | solution.py:18
  98.3 17.9 %collective-permute-start.7 = (bf16[256,768]{1,0:T(8,128)(2,1)S(1)}, bf16[256,768]{1,0:T(8,128)(2,1)S(1)}, u32[]{:S(2)}, u32[]{:S(2)}) collective-permute-start(bf16[256,768]{1,0:T(8,128)(2,1)S(1)} %get-tuple-element.148), channel_id=1, source_target_pairs={{0,3},{1,0},{2,1},{3,2},{4,7},{5,4},{6,5},{7,6},{8,11},{9,8},{10,9... | collective-permute-start | bytes 1179656 | tf_op jit(solution)/shard_map/ppermute | solution.py:21
  106.2 14.4 %collective-permute-start.2 = (bf16[256,768]{1,0:T(8,128)(2,1)S(1)}, bf16[256,768]{1,0:T(8,128)(2,1)S(1)}, u32[]{:S(2)}, u32[]{:S(2)}) collective-permute-start(bf16[256,768]{1,0:T(8,128)(2,1)S(1)} %collective-permute-done), channel_id=1, source_target_pairs={{0,1},{1,2},{2,3},{3,0},{4,5},{5,6},{6,7},{7,4},{8,9},{9,10},{10,1... | collective-permute-start | bytes 1179656 | tf_op jit(solution)/shard_map/ppermute | solution.py:18
  114.7 19.8 %collective-permute-start.8 = (bf16[256,768]{1,0:T(8,128)(2,1)S(1)}, bf16[256,768]{1,0:T(8,128)(2,1)S(1)}, u32[]{:S(2)}, u32[]{:S(2)}) collective-permute-start(bf16[256,768]{1,0:T(8,128)(2,1)S(1)} %collective-permute-done.6), channel_id=1, source_target_pairs={{0,1},{1,2},{2,3},{3,0},{4,5},{5,6},{6,7},{7,4},{8,9},{9,10},{10,1... | collective-permute-start | bytes 1179656 | tf_op jit(solution)/shard_map/ppermute | solution.py:18
  134.0 56.0 %reduce-scatter.17.cloned.1.call-start = ((), (), s32[]{:S(2)}) async-start(), calls=%async_computation.19 | async-start | bytes 1966080 | tf_op jit(solution)/shard_map/reduce_scatter | solution.py:52
  149.6 73.0 %all-gather.3.cloned.1.call-start = ((), (), s32[]{:S(2)}) async-start(), calls=%async_computation.16 | async-start | bytes 1327104 | tf_op jit(solution)/shard_map/all_gather | solution.py:119
  150.2 94.8 %all-gather.5.cloned.1.call-start = ((), (), s32[]{:S(2)}) async-start(), calls=%async_computation.17 | async-start | bytes 1327104 | tf_op jit(solution)/shard_map/all_gather | solution.py:120
  193.3 8.3 %collective-permute-start.3 = (bf16[256,768]{1,0:T(8,128)(2,1)}, bf16[256,768]{1,0:T(8,128)(2,1)}, u32[]{:S(2)}, u32[]{:S(2)}) collective-permute-start(bf16[256,768]{1,0:T(8,128)(2,1)} %get-tuple-element.128), channel_id=1, source_target_pairs={{0,1},{1,2},{2,3},{3,0},{4,5},{5,6},{6,7},{7,4},{8,9},{9,10},{10,1... | collective-permute-start | bytes 1179656 | tf_op jit(solution)/shard_map/ppermute | solution.py:18
  196.1 14.0 %collective-permute-start.9 = (bf16[256,768]{1,0:T(8,128)(2,1)}, bf16[256,768]{1,0:T(8,128)(2,1)}, u32[]{:S(2)}, u32[]{:S(2)}) collective-permute-start(bf16[256,768]{1,0:T(8,128)(2,1)} %get-tuple-element.134), channel_id=1, source_target_pairs={{0,1},{1,2},{2,3},{3,0},{4,5},{5,6},{6,7},{7,4},{8,9},{9,10},{10,1... | collective-permute-start | bytes 1179656 | tf_op jit(solution)/shard_map/ppermute | solution.py:18
  196.5 15.5 %collective-permute-start.4 = (bf16[256,768]{1,0:T(8,128)(2,1)}, bf16[256,768]{1,0:T(8,128)(2,1)}, u32[]{:S(2)}, u32[]{:S(2)}) collective-permute-start(bf16[256,768]{1,0:T(8,128)(2,1)} %get-tuple-element.128), channel_id=1, source_target_pairs={{0,3},{1,0},{2,1},{3,2},{4,7},{5,4},{6,5},{7,6},{8,11},{9,8},{10,9... | collective-permute-start | bytes 1179656 | tf_op jit(solution)/shard_map/ppermute | solution.py:21
  197.8 18.2 %collective-permute-start.10 = (bf16[256,768]{1,0:T(8,128)(2,1)}, bf16[256,768]{1,0:T(8,128)(2,1)}, u32[]{:S(2)}, u32[]{:S(2)}) collective-permute-start(bf16[256,768]{1,0:T(8,128)(2,1)} %get-tuple-element.134), channel_id=1, source_target_pairs={{0,3},{1,0},{2,1},{3,2},{4,7},{5,4},{6,5},{7,6},{8,11},{9,8},{10,9... | collective-permute-start | bytes 1179656 | tf_op jit(solution)/shard_map/ppermute | solution.py:21
  198.3 80.1 %reduce-scatter.15.cloned.1.call-start = ((), (), s32[]{:S(2)}) async-start(), calls=%async_computation.18 | async-start | bytes 1966080 | tf_op jit(solution)/shard_map/reduce_scatter | solution.py:52
  201.7 16.2 %collective-permute-start.5 = (bf16[256,768]{1,0:T(8,128)(2,1)}, bf16[256,768]{1,0:T(8,128)(2,1)S(1)}, u32[]{:S(2)}, u32[]{:S(2)}) collective-permute-start(bf16[256,768]{1,0:T(8,128)(2,1)} %collective-permute-done.3), channel_id=1, source_target_pairs={{0,1},{1,2},{2,3},{3,0},{4,5},{5,6},{6,7},{7,4},{8,9},{9,10},{10,1... | collective-permute-start | bytes 1179656 | tf_op jit(solution)/shard_map/ppermute | solution.py:18
  210.1 11.7 %collective-permute-start.11 = (bf16[256,768]{1,0:T(8,128)(2,1)}, bf16[256,768]{1,0:T(8,128)(2,1)S(1)}, u32[]{:S(2)}, u32[]{:S(2)}) collective-permute-start(bf16[256,768]{1,0:T(8,128)(2,1)} %collective-permute-done.9), channel_id=1, source_target_pairs={{0,1},{1,2},{2,3},{3,0},{4,5},{5,6},{6,7},{7,4},{8,9},{9,10},{10,1... | collective-permute-start | bytes 1179656 | tf_op jit(solution)/shard_map/ppermute | solution.py:18
  249.3 58.7 %reduce-scatter.19.cloned.1.call-start = ((), (), s32[]{:S(2)}) async-start(), calls=%async_computation.20 | async-start | bytes 1966080 | tf_op jit(solution)/shard_map/reduce_scatter | solution.py:52
  253.8 131.7 %reduce-scatter.25.cloned.1.call-start = ((), (), s32[]{:S(2)}) async-start(), calls=%async_computation.23 | async-start | bytes 1966080 | tf_op jit(solution)/shard_map/reduce_scatter | solution.py:52
  314.3 9.5 %collective-permute-start.18 = (bf16[256,768]{1,0:T(8,128)(2,1)S(1)}, bf16[256,768]{1,0:T(8,128)(2,1)S(1)}, u32[]{:S(2)}, u32[]{:S(2)}) collective-permute-start(bf16[256,768]{1,0:T(8,128)(2,1)S(1)} %get-tuple-element.119), channel_id=1, source_target_pairs={{0,1},{1,2},{2,3},{3,0},{4,5},{5,6},{6,7},{7,4},{8,9},{9,10},{10,1... | collective-permute-start | bytes 1179656 | tf_op jit(solution)/shard_map/ppermute | solution.py:18
  315.7 16.5 %collective-permute-start.12 = (bf16[256,768]{1,0:T(8,128)(2,1)S(1)}, bf16[256,768]{1,0:T(8,128)(2,1)S(1)}, u32[]{:S(2)}, u32[]{:S(2)}) collective-permute-start(bf16[256,768]{1,0:T(8,128)(2,1)S(1)} %get-tuple-element.121), channel_id=1, source_target_pairs={{0,1},{1,2},{2,3},{3,0},{4,5},{5,6},{6,7},{7,4},{8,9},{9,10},{10,1... | collective-permute-start | bytes 1179656 | tf_op jit(solution)/shard_map/ppermute | solution.py:18
  316.1 16.4 %collective-permute-start.19 = (bf16[256,768]{1,0:T(8,128)(2,1)S(1)}, bf16[256,768]{1,0:T(8,128)(2,1)S(1)}, u32[]{:S(2)}, u32[]{:S(2)}) collective-permute-start(bf16[256,768]{1,0:T(8,128)(2,1)S(1)} %get-tuple-element.119), channel_id=1, source_target_pairs={{0,3},{1,0},{2,1},{3,2},{4,7},{5,4},{6,5},{7,6},{8,11},{9,8},{10,9... | collective-permute-start | bytes 1179656 | tf_op jit(solution)/shard_map/ppermute | solution.py:21
  317.4 17.9 %collective-permute-start.13 = (bf16[256,768]{1,0:T(8,128)(2,1)S(1)}, bf16[256,768]{1,0:T(8,128)(2,1)S(1)}, u32[]{:S(2)}, u32[]{:S(2)}) collective-permute-start(bf16[256,768]{1,0:T(8,128)(2,1)S(1)} %get-tuple-element.121), channel_id=1, source_target_pairs={{0,3},{1,0},{2,1},{3,2},{4,7},{5,4},{6,5},{7,6},{8,11},{9,8},{10,9... | collective-permute-start | bytes 1179656 | tf_op jit(solution)/shard_map/ppermute | solution.py:21
  323.8 20.4 %collective-permute-start.20 = (bf16[256,768]{1,0:T(8,128)(2,1)S(1)}, bf16[256,768]{1,0:T(8,128)(2,1)S(1)}, u32[]{:S(2)}, u32[]{:S(2)}) collective-permute-start(bf16[256,768]{1,0:T(8,128)(2,1)S(1)} %collective-permute-done.18), channel_id=1, source_target_pairs={{0,1},{1,2},{2,3},{3,0},{4,5},{5,6},{6,7},{7,4},{8,9},{9,10},{10,1... | collective-permute-start | bytes 1179656 | tf_op jit(solution)/shard_map/ppermute | solution.py:18
  332.2 10.4 %collective-permute-start.14 = (bf16[256,768]{1,0:T(8,128)(2,1)S(1)}, bf16[256,768]{1,0:T(8,128)(2,1)S(1)}, u32[]{:S(2)}, u32[]{:S(2)}) collective-permute-start(bf16[256,768]{1,0:T(8,128)(2,1)S(1)} %collective-permute-done.12), channel_id=1, source_target_pairs={{0,1},{1,2},{2,3},{3,0},{4,5},{5,6},{6,7},{7,4},{8,9},{9,10},{10,1... | collective-permute-start | bytes 1179656 | tf_op jit(solution)/shard_map/ppermute | solution.py:18
  357.3 58.6 %reduce-scatter.21.cloned.1.call-start = ((), (), s32[]{:S(2)}) async-start(), calls=%async_computation.21 | async-start | bytes 1966080 | tf_op jit(solution)/shard_map/reduce_scatter | solution.py:52
  361.7 162.7 %reduce-scatter.23.cloned.1.call-start = ((), (), s32[]{:S(2)}) async-start(), calls=%async_computation.22 | async-start | bytes 1966080 | tf_op jit(solution)/shard_map/reduce_scatter | solution.py:52
  421.3 9.8 %collective-permute-start.15 = (bf16[256,768]{1,0:T(8,128)(2,1)S(1)}, bf16[256,768]{1,0:T(8,128)(2,1)S(1)}, u32[]{:S(2)}, u32[]{:S(2)}) collective-permute-start(bf16[256,768]{1,0:T(8,128)(2,1)S(1)} %get-tuple-element.115), channel_id=1, source_target_pairs={{0,1},{1,2},{2,3},{3,0},{4,5},{5,6},{6,7},{7,4},{8,9},{9,10},{10,1... | collective-permute-start | bytes 1179656 | tf_op jit(solution)/shard_map/ppermute | solution.py:18
  422.3 17.3 %collective-permute-start.21 = (bf16[256,768]{1,0:T(8,128)(2,1)S(1)}, bf16[256,768]{1,0:T(8,128)(2,1)}, u32[]{:S(2)}, u32[]{:S(2)}) collective-permute-start(bf16[256,768]{1,0:T(8,128)(2,1)S(1)} %get-tuple-element.117), channel_id=1, source_target_pairs={{0,1},{1,2},{2,3},{3,0},{4,5},{5,6},{6,7},{7,4},{8,9},{9,10},{10,1... | collective-permute-start | bytes 1179656 | tf_op jit(solution)/shard_map/ppermute | solution.py:18
  422.4 18.8 %collective-permute-start.16 = (bf16[256,768]{1,0:T(8,128)(2,1)S(1)}, bf16[256,768]{1,0:T(8,128)(2,1)S(1)}, u32[]{:S(2)}, u32[]{:S(2)}) collective-permute-start(bf16[256,768]{1,0:T(8,128)(2,1)S(1)} %get-tuple-element.115), channel_id=1, source_target_pairs={{0,3},{1,0},{2,1},{3,2},{4,7},{5,4},{6,5},{7,6},{8,11},{9,8},{10,9... | collective-permute-start | bytes 1179656 | tf_op jit(solution)/shard_map/ppermute | solution.py:21
  424.2 17.9 %collective-permute-start.22 = (bf16[256,768]{1,0:T(8,128)(2,1)S(1)}, bf16[256,768]{1,0:T(8,128)(2,1)S(1)}, u32[]{:S(2)}, u32[]{:S(2)}) collective-permute-start(bf16[256,768]{1,0:T(8,128)(2,1)S(1)} %get-tuple-element.117), channel_id=1, source_target_pairs={{0,3},{1,0},{2,1},{3,2},{4,7},{5,4},{6,5},{7,6},{8,11},{9,8},{10,9... | collective-permute-start | bytes 1179656 | tf_op jit(solution)/shard_map/ppermute | solution.py:21
  431.1 14.3 %collective-permute-start.17 = (bf16[256,768]{1,0:T(8,128)(2,1)S(1)}, bf16[256,768]{1,0:T(8,128)(2,1)S(1)}, u32[]{:S(2)}, u32[]{:S(2)}) collective-permute-start(bf16[256,768]{1,0:T(8,128)(2,1)S(1)} %collective-permute-done.15), channel_id=1, source_target_pairs={{0,1},{1,2},{2,3},{3,0},{4,5},{5,6},{6,7},{7,4},{8,9},{9,10},{10,1... | collective-permute-start | bytes 1179656 | tf_op jit(solution)/shard_map/ppermute | solution.py:18
  439.6 28.8 %collective-permute-start.23 = (bf16[256,768]{1,0:T(8,128)(2,1)}, bf16[256,768]{1,0:T(8,128)(2,1)}, u32[]{:S(2)}, u32[]{:S(2)}) collective-permute-start(bf16[256,768]{1,0:T(8,128)(2,1)} %collective-permute-done.21), channel_id=1, source_target_pairs={{0,1},{1,2},{2,3},{3,0},{4,5},{5,6},{6,7},{7,4},{8,9},{9,10},{10,1... | collective-permute-start | bytes 1179656 | tf_op jit(solution)/shard_map/ppermute | solution.py:18
  473.1 58.8 %reduce-scatter.27.cloned.1.call-start = ((), (), s32[]{:S(2)}) async-start(), calls=%async_computation.24 | async-start | bytes 1966080 | tf_op jit(solution)/shard_map/reduce_scatter | solution.py:52
  499.2 106.0 %reduce-scatter.35.cloned.1.call-start = ((), (), s32[]{:S(2)}) async-start(), calls=%async_computation.28 | async-start | bytes 1327104 | tf_op jit(solution)/shard_map/reduce_scatter | solution.py:58
  505.4 166.9 %reduce-scatter.33.cloned.1.call-start = ((), (), s32[]{:S(2)}) async-start(), calls=%async_computation.27 | async-start | bytes 1327104 | tf_op jit(solution)/shard_map/reduce_scatter | solution.py:58
  511.8 225.0 %reduce-scatter.31.cloned.1.call-start = ((), (), s32[]{:S(2)}) async-start(), calls=%async_computation.26 | async-start | bytes 442368 | tf_op jit(solution)/shard_map/reduce_scatter | solution.py:58
  518.8 284.3 %reduce-scatter.29.cloned.1.call-start = ((), (), s32[]{:S(2)}) async-start(), calls=%async_computation.25 | async-start | bytes 1105920 | tf_op jit(solution)/shard_map/reduce_scatter | solution.py:58
  535.7 138.4 %copy-start.83 = (f32[768]{0:T(1024)S(1)}, f32[768]{0:T(1024)}, u32[]{:S(2)}) copy-start(f32[768]{0:T(1024)} %get-tuple-element.86) | copy-start | bytes 9220
  535.7 138.4 %copy-start.84 = (f32[768]{0:T(1024)S(1)}, f32[768]{0:T(1024)}, u32[]{:S(2)}) copy-start(f32[768]{0:T(1024)} %get-tuple-element.87) | copy-start | bytes 9220
  535.7 138.5 %copy-start.81 = (f32[768]{0:T(1024)S(1)}, f32[768]{0:T(1024)}, u32[]{:S(2)}) copy-start(f32[768]{0:T(1024)} %get-tuple-element.77) | copy-start | bytes 9220
  535.7 138.5 %copy-start.82 = (f32[768]{0:T(1024)S(1)}, f32[768]{0:T(1024)}, u32[]{:S(2)}) copy-start(f32[768]{0:T(1024)} %get-tuple-element.90) | copy-start | bytes 9220
  535.7 138.6 %copy-start.86 = (f32[768]{0:T(1024)S(1)}, f32[768]{0:T(1024)}, u32[]{:S(2)}) copy-start(f32[768]{0:T(1024)} %get-tuple-element.112) | copy-start | bytes 9220
  535.7 138.6 %copy-start.87 = (f32[768]{0:T(1024)S(1)}, f32[768]{0:T(1024)}, u32[]{:S(2)}) copy-start(f32[768]{0:T(1024)} %get-tuple-element.143) | copy-start | bytes 9220
  535.7 138.7 %copy-start.66 = (f32[32,24]{1,0:T(8,128)S(1)}, f32[32,24]{1,0:T(8,128)}, u32[]{:S(2)}) copy-start(f32[32,24]{1,0:T(8,128)} %add.450) | copy-start | bytes 9220
  535.7 138.8 %copy-start.47 = (bf16[3,64,1024]{2,1,0:T(8,128)(2,1)S(1)}, bf16[3,64,1024]{2,1,0:T(8,128)(2,1)}, u32[]{:S(2)}) copy-start(bf16[3,64,1024]{2,1,0:T(8,128)(2,1)} %copy-done.45) | copy-start | bytes 1179652
  535.8 268.9 %all-to-all-start.2 = ((bf16[256,2,768]{2,1,0:T(2,128)(2,1)}), bf16[256,2,768]{2,1,0:T(2,128)(2,1)S(1)}, u32[]{:S(2)}, u32[]{:S(2)}) async-start(bf16[256,2,768]{2,1,0:T(2,128)(2,1)} %copy.91), calls=%async_computation.10 | async-start | bytes 1572864 | tf_op jit(solution)/shard_map/all_to_all | solution.py:370
  (103 other events, 1227.5 us)
Sparse Core Ops, SparseCore 0:
  134.1 25.1 reduce-scatter.12
  161.8 28.0 reduce-scatter.16
  249.4 28.0 reduce-scatter.14
  279.9 28.0 reduce-scatter.18
  357.4 27.9 reduce-scatter.24
  387.9 27.9 reduce-scatter.20
  473.2 28.0 reduce-scatter.22
  503.8 27.9 reduce-scatter.26
  535.2 69.9 reduce-scatter.34
  608.5 63.7 reduce-scatter.32
  675.6 61.1 reduce-scatter.30
  740.0 63.0 reduce-scatter.28
Sparse Core Ops, SparseCore 1:
  152.3 38.6 all-gather.2
  198.4 41.3 all-gather.4
